TPU v7x, 32 devices: a whole 2x2x4 slice. The times are simulated.
32 devices in a mesh: fsdp: 8 (over z, x), tp: 4 (over y, core).
Axes of the slice: x: 2, y: 2, z: 4, core: 2. Of those that a mesh axis runs over, the one named last changes fastest.
Arguments:
- slopes_in: float32 [32, 128, 4096], P(None, 'fsdp', 'tp'), may hold values from -6 to 6
- moments_in: float32 [32, 128, 4096], P(None, 'fsdp', 'tp'), may hold values from -6 to 6
- weights_in: float32 [32, 128, 4096], P(None, 'fsdp', 'tp'), may hold values from -0.1875 to 0.1875
Outputs:
- new_weights: float32 [32, 128, 4096], P(None, 'fsdp', 'tp')
- new_momentum: float32 [32, 128, 4096], P(None, 'fsdp', 'tp')
All inputs are finite; a program needn't handle non-finite values.
Results may differ from a plain program's by a relative error of at most 0.00021.
Values sent between devices are 32-bit elements; how exact they have to be, the bound alone decides.
A program may use at most 128 MiB of HBM per device.

v0:
```python
import jax
import jax.numpy as jnp
from jax import lax
from jax.sharding import PartitionSpec as P

ITERS = 5


hold_rate = 0.8
learn_rate = 1.0


def body(slopes_in, moments_in, weights_in):
    new_momentum = hold_rate * moments_in + slopes_in
    moved = lax.all_to_all(new_momentum, "fsdp", split_axis=0, concat_axis=1, tiled=True)
    whole = lax.all_to_all(moved, "tp", split_axis=0, concat_axis=2, tiled=True)
    iterate = whole * lax.rsqrt(jnp.sum(whole * whole, axis=(1, 2), keepdims=True) + 1e-06)
    for step in range(ITERS):
        gram = jnp.einsum("mik,mjk->mij", iterate, iterate, precision=lax.Precision.HIGHEST)
        mixed = -4.775 * gram + 2.0315 * jnp.einsum(
            "mij,mjk->mik", gram, gram, precision=lax.Precision.HIGHEST
        )
        iterate = 3.4445 * iterate + jnp.einsum(
            "mij,mjk->mik", mixed, iterate, precision=lax.Precision.HIGHEST
        )
    iterate = lax.all_to_all(iterate, "tp", split_axis=2, concat_axis=0, tiled=True)
    back = lax.all_to_all(iterate, "fsdp", split_axis=1, concat_axis=0, tiled=True)
    new_weights = weights_in - learn_rate * back
    return (new_weights, new_momentum)


def solution(mesh):
    return jax.shard_map(
        body,
        mesh=mesh,
        in_specs=(P(None, "fsdp", "tp"), P(None, "fsdp", "tp"), P(None, "fsdp", "tp")),
        out_specs=(P(None, "fsdp", "tp"), P(None, "fsdp", "tp")),
        check_vma=False,
    )
```

profile of v0, /device:TPU:0, one launch (start us, length us, event | category | flops | bytes accessed | tf_op | source)
XLA Modules:
  0.0 212.4 jit_solution(16108924228545123372)
XLA Ops:
  0.6 2.7 %multiply_add_fusion = f32[32,16,1024]{2,1,0:T(8,128)S(1)} fusion(f32[32,16,1024]{2,1,0:T(8,128)} %param.3, f32[32,16,1024]{2,1,0:T(8,128)} %param.4), kind=kLoop, calls=%fused_computation.11 | loop fusion | flops 1048576 | bytes 6291456 | tf_op jit(solution)/shard_map/add | solution.py:14
  3.3 55.3 %all_to_all.63 = f32[32,16,1024]{2,1,0:T(8,128)S(1)} all-to-all(f32[32,16,1024]{2,1,0:T(8,128)S(1)} %multiply_add_fusion), channel_id=1, replica_groups=mesh['fsdp'=8,'tp'=4] {'fsdp'}, dimensions={0} | all-to-all | bytes 4194304 | tf_op jit(solution)/shard_map/all_to_all | solution.py:15
  58.9 28.3 %all_to_all.64 = f32[4,128,1024]{2,1,0:T(8,128)S(1)} all-to-all(f32[4,128,1024]{2,1,0:T(8,128)S(1)} %bitcast.63), channel_id=1, replica_groups=mesh['fsdp'=8,'tp'=4] {'tp'}, dimensions={0} | all-to-all | bytes 4194304 | tf_op jit(solution)/shard_map/all_to_all | solution.py:16
  88.9 1.8 fusion.4
  91.0 2.6 %multiply_bitcast_fusion.1 = (f32[1,128,4,1024]{3,1,2,0:T(8,128)}, f32[1,128,4,1024]{3,1,2,0:T(8,128)}) fusion(f32[4,128,1024]{2,1,0:T(8,128)S(1)} %all_to_all.64, f32[]{:T(128)S(6)} %rsqrt.4), kind=kLoop, calls=%fused_computation.13 | loop fusion | flops 1048576 | bytes 6291460 | tf_op jit(solution)/shard_map/mul | solution.py:17
  93.5 1.9 copy.32
  95.4 2.9 %copy.31 = f32[1,128,4,1024]{1,3,2,0:T(8,128)} copy(f32[1,128,4,1024]{3,1,2,0:T(8,128)} %get-tuple-element.3) | data formatting | bytes 4194304 | tf_op jit(solution)/shard_map/mul | solution.py:23
  98.3 3.0 %copy.33 = f32[128,4096]{1,0:T(8,128)} copy(f32[128,4096]{0,1:T(8,128)} %bitcast.64) | data formatting | bytes 4194304 | tf_op jit(solution)/shard_map/mul | solution.py:23
  101.3 3.6 %convolution_add_fusion.4 = f32[128,4096]{1,0:T(8,128)S(1)} fusion(f32[128,4096]{1,0:T(8,128)} %copy.33, f32[128,128]{1,0:T(8,128)S(1)} %fusion.11, f32[128,4096]{0,1:T(8,128)S(1)} %bitcast.62), kind=kOutput, calls=%fused_computation.5 | convolution fusion | flops 805830656 | bytes 6356992 | tf_op jit(solution)/shard_map/mij,mjk->mik/dot_general | solution.py:23
  104.9 1.8 fusion.13
  106.9 2.0 convolution_add_fusion.3
  108.9 1.8 fusion.14
  110.9 2.0 convolution_add_fusion.2
  113.0 1.8 fusion.15
  115.0 2.3 %convolution_add_fusion.1 = f32[128,4096]{1,0:T(8,128)S(1)} fusion(f32[128,128]{1,0:T(8,128)S(1)} %fusion.8, f32[128,4096]{1,0:T(8,128)S(1)} %convolution_add_fusion.2), kind=kOutput, calls=%fused_computation.2 | convolution fusion | flops 806354944 | bytes 4259840 | tf_op jit(solution)/shard_map/mij,mjk->mik/dot_general | solution.py:23
  117.3 1.8 fusion.16
  119.3 2.0 fusion
  121.3 3.7 %copy.34 = f32[1,128,4096]{1,0,2:T(1,128)} copy(f32[1,128,4096]{2,1,0:T(8,128)S(1)} %fusion) | data formatting | bytes 4194304 | tf_op jit(solution)/shard_map/add | solution.py:23
  125.0 29.2 %all_to_all.65 = f32[1,128,4096]{1,0,2:T(1,128)S(1)} all-to-all(f32[1,128,4096]{1,0,2:T(1,128)} %copy.34), channel_id=1, replica_groups=mesh['fsdp'=8,'tp'=4] {'tp'}, dimensions={2} | all-to-all | bytes 4194304 | tf_op jit(solution)/shard_map/all_to_all | solution.py:26
  154.3 2.0 copy.35
  156.2 51.7 %all_to_all.66 = f32[4,128,1024]{2,0,1:T(4,128)S(1)} all-to-all(f32[4,128,1024]{2,0,1:T(4,128)} %copy.35), channel_id=1, replica_groups=mesh['fsdp'=8,'tp'=4] {'fsdp'}, dimensions={1} | all-to-all | bytes 4194304 | tf_op jit(solution)/shard_map/all_to_all | solution.py:27
  207.9 1.2 copy.36
  209.4 1.3 copy-done.1
  210.7 1.7 bitcast_subtract_fusion
  (11 shorter events, 2.7 us)
Async XLA Ops:
  3.3 55.3 %copy-start = (f32[32,16,1024]{2,1,0:T(8,128)}, f32[32,16,1024]{2,1,0:T(8,128)S(1)}, u32[]{:S(2)}) copy-start(f32[32,16,1024]{2,1,0:T(8,128)S(1)} %multiply_add_fusion) | copy-start | bytes 6291460
  209.1 1.6 copy-start.1
where the time goes:
time: 213 us; the launch traced here: 212 us
  blocking collectives  164 us (77%)
  matrix products  22 us (10%)
  local copies, waits for them, and re-layouts  16.4 us (8%)
  other arithmetic  8.09 us (4%)
    all_to_all x1, blocking collectives, body(): lax.all_to_all(new_momentum, 'fsdp', split_axis=0, concat_axis=1, tiled=T...  55.3 us
    all_to_all x1, blocking collectives, body(): lax.all_to_all(iterate, 'fsdp', split_axis=1, concat_axis=0, tiled=True)  51.7 us
    all_to_all x1, blocking collectives, body(): lax.all_to_all(iterate, 'tp', split_axis=2, concat_axis=0, tiled=True)  29.2 us
    all_to_all x1, blocking collectives, body(): whole = lax.all_to_all(moved, 'tp', split_axis=0, concat_axis=2, tiled=True)  28.3 us
    dot_general x5, matrix products, body(): jnp.einsum('mij,mjk->mik', mixed, iterate, precision=lax.Precision.HIGHEST)  12 us
    dot_general x5, matrix products, body(): jnp.einsum('mik,mjk->mij', iterate, iterate, precision=lax.Precision.HIGH...  8.96 us
    mul x2, local copies, waits for them, and re-layouts, body(): 3.4445 * iterate  5.84 us

commit v1 on v0

v1 whole, which is shorter than its diff:
```python
import functools

import jax
import jax.numpy as jnp
from jax import lax
from jax.sharding import PartitionSpec as P

ITERS = 5
HIGH = lax.Precision.HIGHEST


hold_rate = 0.8
learn_rate = 1.0


def polynomial(gram):
    side = gram.shape[-1]
    eye = jnp.eye(side, dtype=gram.dtype)
    dot = functools.partial(jnp.einsum, "mij,mjk->mik", precision=HIGH)
    scale = lax.rsqrt(jnp.sum(gram * eye, axis=(1, 2), keepdims=True) + 1e-06)
    gram = gram * (scale * scale)
    total = None
    for step in range(ITERS):
        mixed = 3.4445 * eye - 4.775 * gram + 2.0315 * dot(gram, gram)
        total = mixed * scale if total is None else dot(mixed, total)
        if step < ITERS - 1:
            gram = dot(dot(mixed, gram), mixed)
    return total


def body(slopes_in, moments_in, weights_in):
    new_momentum = hold_rate * moments_in + slopes_in
    moved = lax.all_to_all(new_momentum, "fsdp", split_axis=0, concat_axis=1, tiled=True)
    gram = lax.psum(jnp.einsum("mik,mjk->mij", moved, moved, precision=HIGH), "tp")
    iterate = jnp.einsum("mij,mjk->mik", polynomial(gram), moved, precision=HIGH)
    back = lax.all_to_all(iterate, "fsdp", split_axis=1, concat_axis=0, tiled=True)
    new_weights = weights_in - learn_rate * back
    return (new_weights, new_momentum)


def solution(mesh):
    return jax.shard_map(
        body,
        mesh=mesh,
        in_specs=(P(None, "fsdp", "tp"), P(None, "fsdp", "tp"), P(None, "fsdp", "tp")),
        out_specs=(P(None, "fsdp", "tp"), P(None, "fsdp", "tp")),
        check_vma=False,
    )
```

time: 213 us -> 176 us (0.83)
  blocking collectives: 164 us -> 108 us
  waiting for transfers between devices: 0 us -> 31.5 us
  local copies, waits for them, and re-layouts: 16.4 us -> 3.08 us
  between operations: 1.48 us -> 14.2 us
  matrix products: 22 us -> 13.5 us
  other arithmetic: 8.09 us -> 5.5 us
    all_to_all x2 -> x0, blocking collectives: 57.5 us -> none  [the longest x1 29.2 us: body(): lax.all_to_all(iterate, 'tp', split_axis=2, concat_axis=0, tiled=True)]
    psum x0 -> x1, waiting for transfers between devices: none -> 31.4 us  [body(): lax.psum(jnp.einsum('mik,mjk->mij', moved, moved, precision=HIGH), 'tp')]
    dot_general x15 -> x19, matrix products: 22 us -> 13.5 us  [the longest x8 4.15 us: polynomial(): gram = dot(dot(mixed, gram), mixed)]
    mul x3 -> x0, local copies, waits for them, and re-layouts: 7.74 us -> none  [the longest x2 5.84 us: body(): 3.4445 * iterate]
    add x1 -> x0, local copies, waits for them, and re-layouts: 3.7 us -> none  [body(): 3.4445 * iterate]
    mul x1, other arithmetic: 2.56 us -> 0.01 us  [polynomial(): mixed = 3.4445 * eye - 4.775 * gram + 2.0315 * dot(gram, gram)]
  transfers between devices with their start and end apart: 0 -> 1, of which waited for: 0 -> 1; matrix products, arithmetic and copies ran while one was open for 0% -> 0% of each run, Pallas kernels for 0% -> 0%
where the time goes in v1:
time: 176 us
  blocking collectives  108 us (61%)
  waiting for transfers between devices  31.5 us (18%)
  between operations  14.2 us (8%)
  matrix products  13.5 us (8%)
  other arithmetic  5.5 us (3%)
  local copies, waits for them, and re-layouts  3.08 us (2%)
    all_to_all x1, blocking collectives, body(): lax.all_to_all(new_momentum, 'fsdp', split_axis=0, concat_axis=1, tiled=T...  55.3 us
    all_to_all x1, blocking collectives, body(): lax.all_to_all(iterate, 'fsdp', split_axis=1, concat_axis=0, tiled=True)  52.5 us
    psum x1, waiting for transfers between devices, body(): lax.psum(jnp.einsum('mik,mjk->mij', moved, moved, precision=HIGH), 'tp')  31.4 us
    dot_general x8, matrix products, polynomial(): gram = dot(dot(mixed, gram), mixed)  4.15 us
  transfers between devices with their start and end apart: 1, of which 1 were waited for; matrix products, arithmetic and copies ran while one was open for 0% of the time, Pallas kernels for 0%

profile of v1, /device:TPU:0, one launch (start us, length us, event | category | flops | bytes accessed | tf_op | source)
XLA Modules:
  0.0 175.6 jit_solution(531279541024470661)
XLA Ops:
  7.2 2.7 %multiply_add_fusion = f32[32,16,1024]{2,1,0:T(8,128)S(1)} fusion(f32[32,16,1024]{2,1,0:T(8,128)} %param.3, f32[32,16,1024]{2,1,0:T(8,128)} %param.4), kind=kLoop, calls=%fused_computation.1 | loop fusion | flops 1048576 | bytes 6291456 | tf_op jit(solution)/shard_map/add | solution.py:32
  9.9 55.3 %all_to_all.36 = f32[32,16,1024]{2,1,0:T(8,128)S(1)} all-to-all(f32[32,16,1024]{2,1,0:T(8,128)S(1)} %multiply_add_fusion), channel_id=1, replica_groups=mesh['fsdp'=8,'tp'=4] {'fsdp'}, dimensions={0} | all-to-all | bytes 4194304 | tf_op jit(solution)/shard_map/all_to_all | solution.py:33
  65.3 2.8 %fusion.16 = f32[4,128,128]{2,1,0:T(8,128)} fusion(f32[4,128,1024]{2,1,0:T(8,128)S(1)} %bitcast.43), kind=kOutput, calls=%fused_computation.26 | convolution fusion | flops 805306368 | bytes 2359296 | tf_op jit(solution)/shard_map/mik,mjk->mij/dot_general | solution.py:34
  68.2 31.4 %all-reduce.2.cloned.1.call-done = f32[4,128,128]{2,1,0:T(8,128)} async-done(((f32[4,128,128]{2,1,0:T(8,128)}), f32[4,128,128]{2,1,0:T(8,128)}) %all-reduce.2.cloned.1.call-update) | async-done | bytes 262160 | tf_op jit(solution)/shard_map/psum | solution.py:34
  99.6 1.1 multiply_reduce_fusion
  100.7 1.6 fusion.4
  102.3 1.4 fusion.8
  103.7 0.4 fusion.17
  104.5 0.4 fusion.18
  104.9 0.4 fusion.5
  105.3 0.4 fusion.19
  106.1 0.4 fusion.20
  106.5 0.4 fusion.24
  106.9 0.4 fusion.21
  107.7 0.4 fusion.22
  108.1 0.4 fusion.25
  108.5 0.4 fusion.23
  109.3 0.4 fusion.26
  109.7 1.9 %fusion.27 = f32[4,128,1024]{2,1,0:T(8,128)S(1)} fusion(f32[4,128,128]{2,1,0:T(8,128)S(1)} %fusion.26, f32[4,128,1024]{2,1,0:T(8,128)S(1)} %bitcast.44), kind=kOutput, calls=%fused_computation.37 | convolution fusion | flops 805306368 | bytes 4456448 | tf_op jit(solution)/shard_map/mij,mjk->mik/dot_general | solution.py:35
  111.6 1.4 copy.8
  113.0 52.5 %all_to_all.37 = f32[4,128,1024]{2,0,1:T(4,128)S(1)} all-to-all(f32[4,128,1024]{2,0,1:T(4,128)S(1)} %copy.8), channel_id=1, replica_groups=mesh['fsdp'=8,'tp'=4] {'fsdp'}, dimensions={1} | all-to-all | bytes 4194304 | tf_op jit(solution)/shard_map/all_to_all | solution.py:36
  165.4 1.2 copy.9
  166.6 0.4 copy-done.1
  167.0 1.7 bitcast_subtract_fusion
  (13 shorter events, 1.7 us)
Async XLA Ops:
  7.2 92.4 %all-reduce.2.cloned.1.call-start = ((), (), s32[]{:S(2)}) async-start(), calls=%async_computation.2 | async-start | bytes 524288 | tf_op jit(solution)/shard_map/psum | solution.py:34
  9.9 55.3 %copy-start = (f32[32,16,1024]{2,1,0:T(8,128)}, f32[32,16,1024]{2,1,0:T(8,128)S(1)}, u32[]{:S(2)}) copy-start(f32[32,16,1024]{2,1,0:T(8,128)S(1)} %multiply_add_fusion) | copy-start | bytes 6291460
  165.4 1.6 copy-start.1
Sparse Core Ops, SparseCore 0:
  68.2 31.3 all-reduce.1

commit v2 on v1

v2 whole, which is shorter than its diff:
```python
import functools

import jax
import jax.numpy as jnp
from jax import lax
from jax.experimental import pallas as pl
from jax.experimental.pallas import tpu as pltpu
from jax.sharding import PartitionSpec as P

ITERS = 5
HIGH = lax.Precision.HIGHEST
MESH = pl.DeviceIdType.MESH


hold_rate = 0.8
learn_rate = 1.0


def polynomial(gram, dot, trace):
    side = gram.shape[-1]
    eye = jnp.where(
        lax.broadcasted_iota(jnp.int32, (side, side), 0) == lax.broadcasted_iota(jnp.int32, (side, side), 1), 1.0, 0.0
    ).astype(gram.dtype)
    scale = lax.rsqrt(trace(gram * eye) + 1e-06)
    gram = gram * (scale * scale)
    total = None
    for step in range(ITERS):
        mixed = 3.4445 * eye - 4.775 * gram + 2.0315 * dot(gram, gram)
        total = mixed * scale if total is None else dot(mixed, total)
        if step < ITERS - 1:
            gram = dot(dot(mixed, gram), mixed)
    return total


def kernel(stages, parts, cols, whole_ref, back_ref, x_ref, y_ref, g_ref, fsend, frecv, bsend, brecv, gsend, grecv, own):
    rows = whole_ref.shape[1]
    side, wide = parts * rows, whole_ref.shape[2]
    f, t = lax.axis_index("fsdp"), lax.axis_index("tp")
    hops = sorted(range(1, parts), key=lambda k: abs(2 * k - parts))

    barrier = pltpu.get_barrier_semaphore()
    for k in range(1, parts):
        pl.semaphore_signal(barrier, inc=1, device_id={"fsdp": lax.rem(f + k, parts)}, device_id_type=MESH)
    for k in range(1, cols):
        pl.semaphore_signal(barrier, inc=1, device_id={"tp": lax.rem(t + k, cols)}, device_id_type=MESH)
    pl.semaphore_wait(barrier, parts + cols - 2)

    def forward(m, peer, sender):
        return pltpu.make_async_remote_copy(
            src_ref=whole_ref.at[m * parts + peer], dst_ref=x_ref.at[m, sender],
            send_sem=fsend.at[m, peer], recv_sem=frecv.at[m, sender],
            device_id={"fsdp": peer}, device_id_type=MESH,
        )

    def backward(m, peer, sender):
        return pltpu.make_async_remote_copy(
            src_ref=y_ref.at[m, peer], dst_ref=back_ref.at[m * parts + sender],
            send_sem=bsend.at[m, peer], recv_sem=brecv.at[m, sender],
            device_id={"fsdp": peer}, device_id_type=MESH,
        )

    def partial(m, peer, sender):
        return pltpu.make_async_remote_copy(
            src_ref=g_ref.at[m, sender], dst_ref=g_ref.at[m, sender],
            send_sem=gsend.at[m, peer], recv_sem=grecv.at[m, sender],
            device_id={"tp": peer}, device_id_type=MESH,
        )

    def take(m):
        return pltpu.make_async_copy(whole_ref.at[m * parts + f], x_ref.at[m, f], own.at[0, m])

    def give(m):
        return pltpu.make_async_copy(y_ref.at[m, f], back_ref.at[m * parts + f], own.at[1, m])

    @pl.loop(0, stages)
    def _(m):
        for k in hops:
            forward(m, lax.rem(f + k, parts), f).start()
        take(m).start()

    dot = functools.partial(jnp.dot, precision=HIGH, preferred_element_type=jnp.float32)

    @pl.loop(0, stages)
    def _(m):
        take(m).wait()
        for k in hops:
            peer = lax.rem(f + k, parts)
            forward(m, peer, peer).wait_recv()
        x = x_ref[m].reshape(side, wide)
        g_ref[m, t] = lax.dot_general(x, x, (((1,), (1,)), ((), ())), precision=HIGH, preferred_element_type=jnp.float32)
        for k in range(1, cols):
            partial(m, lax.rem(t + k, cols), t).start()
        for k in range(1, cols):
            peer = lax.rem(t + k, cols)
            partial(m, peer, peer).wait_recv()
        gram = g_ref[m, 0]
        for k in range(1, cols):
            gram = gram + g_ref[m, k]
        total = polynomial(gram, dot, lambda a: jnp.sum(jnp.sum(a, axis=1, keepdims=True), axis=0, keepdims=True))
        y_ref[m] = dot(total, x_ref[m].reshape(side, wide)).reshape(parts, rows, wide)
        for k in hops:
            backward(m, lax.rem(f + k, parts), f).start()
        give(m).start()

    @pl.loop(0, stages)
    def _(m):
        give(m).wait()
        for k in hops:
            peer = lax.rem(f + k, parts)
            forward(m, peer, f).wait_send()
            backward(m, peer, f).wait_send()
            backward(m, peer, peer).wait_recv()
        for k in range(1, cols):
            partial(m, lax.rem(t + k, cols), t).wait_send()


def iterate_kernel(new_momentum, parts, cols):
    mats, rows, wide = new_momentum.shape
    stages, side = mats // parts, rows * parts
    dma = pltpu.SemaphoreType.DMA
    return pl.pallas_call(
        functools.partial(kernel, stages, parts, cols),
        out_shape=jax.ShapeDtypeStruct(new_momentum.shape, new_momentum.dtype),
        in_specs=[pl.BlockSpec(memory_space=pl.ANY)],
        out_specs=pl.BlockSpec(memory_space=pl.ANY),
        scratch_shapes=[
            pltpu.VMEM((stages, parts, rows, wide), jnp.float32),
            pltpu.VMEM((stages, parts, rows, wide), jnp.float32),
            pltpu.VMEM((stages, cols, side, side), jnp.float32),
            dma((stages, parts)), dma((stages, parts)), dma((stages, parts)), dma((stages, parts)),
            dma((stages, cols)), dma((stages, cols)), dma((2, stages)),
        ],
        compiler_params=pltpu.CompilerParams(collective_id=0, has_side_effects=True),
    )(new_momentum)


def iterate_plain(new_momentum):
    moved = lax.all_to_all(new_momentum, "fsdp", split_axis=0, concat_axis=1, tiled=True)
    gram = lax.psum(jnp.einsum("mik,mjk->mij", moved, moved, precision=HIGH), "tp")
    dot = functools.partial(jnp.einsum, "mij,mjk->mik", precision=HIGH)
    total = polynomial(gram, dot, lambda a: jnp.sum(a, axis=(1, 2), keepdims=True))
    return lax.all_to_all(dot(total, moved), "fsdp", split_axis=1, concat_axis=0, tiled=True)


def body(parts, cols, slopes_in, moments_in, weights_in):
    new_momentum = hold_rate * moments_in + slopes_in
    if new_momentum.shape[1] % 8 == 0:
        back = iterate_kernel(new_momentum, parts, cols)
    else:
        back = iterate_plain(new_momentum)
    new_weights = weights_in - learn_rate * back
    return (new_weights, new_momentum)


def solution(mesh):
    return jax.shard_map(
        functools.partial(body, mesh.shape["fsdp"], mesh.shape["tp"]),
        mesh=mesh,
        in_specs=(P(None, "fsdp", "tp"), P(None, "fsdp", "tp"), P(None, "fsdp", "tp")),
        out_specs=(P(None, "fsdp", "tp"), P(None, "fsdp", "tp")),
        check_vma=False,
    )
```

time: 176 us -> 106 us (0.60)
  blocking collectives: 108 us -> 0 us
  Pallas kernels: 0 us -> 97.3 us
  waiting for transfers between devices: 31.5 us -> 0 us
  between operations: 14.2 us -> 0.65 us
  matrix products: 13.5 us -> 0 us
  local copies, waits for them, and re-layouts: 3.08 us -> 0.01 us
  other arithmetic: 5.5 us -> 7.46 us
    all_to_all x2 -> x0, blocking collectives: 108 us -> none  [the longest x1 55.3 us: body(): lax.all_to_all(new_momentum, 'fsdp', split_axis=0, concat_axis=1, tiled=T...]
    pallas_call x0 -> x1, Pallas kernels: none -> 97.3 us  [iterate_kernel(): pl.pallas_call(functools.partial(kernel, stages, parts, cols), out_shape=...]
    psum x1 -> x0, waiting for transfers between devices: 31.4 us -> none  [body(): lax.psum(jnp.einsum('mik,mjk->mij', moved, moved, precision=HIGH), 'tp')]
    dot_general x19 -> x0, matrix products: 13.5 us -> none  [the longest x8 4.15 us: polynomial(): gram = dot(dot(mixed, gram), mixed)]
  transfers between devices with their start and end apart: 1 -> 0, of which waited for: 1 -> 0; matrix products, arithmetic and copies ran while one was open for 0% -> 0% of each run, Pallas kernels for 0% -> 0%
where the time goes in v2:
time: 106 us; the launch traced here: 105 us
  Pallas kernels  97.3 us (92%)
  other arithmetic  7.46 us (7%)
    pallas_call x1, Pallas kernels, iterate_kernel(): pl.pallas_call(functools.partial(kernel, stages, parts, cols), out_shape=...  97.3 us
    add x1, other arithmetic, body(): new_momentum = hold_rate * moments_in + slopes_in  4.16 us
    sub x1, other arithmetic, body(): new_weights = weights_in - learn_rate * back  3.3 us

profile of v2, /device:TPU:0, one launch (start us, length us, event | category | flops | bytes accessed | tf_op | source)
XLA Modules:
  0.0 105.4 jit_solution(13635871280148618757)
XLA Ops:
  0.6 4.2 %multiply_add_fusion.whole_ref = f32[32,16,1024]{2,1,0:T(8,128)} fusion(f32[32,16,1024]{2,1,0:T(8,128)} %param.3, f32[32,16,1024]{2,1,0:T(8,128)} %param.4), kind=kLoop, calls=%fused_computation | loop fusion | flops 1048576 | bytes 6291456 | tf_op jit(solution)/shard_map/add | solution.py:146
  4.8 0.0 copy-start
  4.8 97.3 %shard_map.50 = f32[32,16,1024]{2,1,0:T(8,128)} custom-call(f32[32,16,1024]{2,1,0:T(8,128)} %multiply_add_fusion.whole_ref), custom_call_target="tpu_custom_call" | custom-call | tf_op jit(solution)/shard_map/pallas_call | solution.py:121
  102.1 0.0 copy-done
  102.1 3.3 %sub.3 = f32[32,16,1024]{2,1,0:T(8,128)} subtract(f32[32,16,1024]{2,1,0:T(8,128)S(1)} %copy-done, f32[32,16,1024]{2,1,0:T(8,128)} %shard_map.50) | non-fusion elementwise | flops 524288 | bytes 6291456 | tf_op jit(solution)/shard_map/sub | solution.py:151
Async XLA Ops:
  4.8 97.3 %copy-start = (f32[32,16,1024]{2,1,0:T(8,128)S(1)}, f32[32,16,1024]{2,1,0:T(8,128)}, u32[]{:S(2)}) copy-start(f32[32,16,1024]{2,1,0:T(8,128)} %param.5) | copy-start | bytes 6291460

commit v3 on v2

--- a/solution.py
+++ b/solution.py
@@ -32,19 +32,29 @@
     return total
 
 
-def kernel(stages, parts, cols, whole_ref, back_ref, x_ref, y_ref, g_ref, fsend, frecv, bsend, brecv, gsend, grecv, own):
+def kernel(
+    stages, parts, cols, slopes_ref, moments_ref, weights_ref, momentum_ref, new_ref,
+    s_ref, m_ref, w_ref, back_ref, whole_ref, x_ref, y_ref, g_ref, fsend, frecv, bsend, brecv, gsend, grecv, own, out,
+):
     rows = whole_ref.shape[1]
     side, wide = parts * rows, whole_ref.shape[2]
     f, t = lax.axis_index("fsdp"), lax.axis_index("tp")
     hops = sorted(range(1, parts), key=lambda k: abs(2 * k - parts))
 
+    def load(m, which, src, dst):
+        some = pl.ds(m * parts, parts)
+        return pltpu.make_async_copy(src.at[some], dst.at[some], own.at[which, m])
+
+    @pl.loop(0, stages)
+    def _(m):
+        load(m, 2, slopes_ref, s_ref).start()
+        load(m, 3, moments_ref, m_ref).start()
+
     barrier = pltpu.get_barrier_semaphore()
     for k in range(1, parts):
-        pl.semaphore_signal(barrier, inc=1, device_id={"fsdp": lax.rem(f + k, parts)}, device_id_type=MESH)
+        pl.semaphore_signal(barrier, inc=1, device_id={"fsdp": lax.rem(f + parts + k * (1 - 2 * lax.rem(t, 2)), parts)}, device_id_type=MESH)
     for k in range(1, cols):
         pl.semaphore_signal(barrier, inc=1, device_id={"tp": lax.rem(t + k, cols)}, device_id_type=MESH)
-    pl.semaphore_wait(barrier, parts + cols - 2)
-
     def forward(m, peer, sender):
         return pltpu.make_async_remote_copy(
             src_ref=whole_ref.at[m * parts + peer], dst_ref=x_ref.at[m, sender],
@@ -67,16 +77,40 @@
         )
 
     def take(m):
-        return pltpu.make_async_copy(whole_ref.at[m * parts + f], x_ref.at[m, f], own.at[0, m])
+        return pltpu.make_async_copy(whole_ref.at[m * parts + f], x_ref.at[m, f], own.at[5, m])
 
     def give(m):
         return pltpu.make_async_copy(y_ref.at[m, f], back_ref.at[m * parts + f], own.at[1, m])
 
-    @pl.loop(0, stages)
-    def _(m):
-        for k in hops:
-            forward(m, lax.rem(f + k, parts), f).start()
+    def put(m, peer):
+        mat = m * parts + peer
+        return pltpu.make_async_copy(w_ref.at[mat], new_ref.at[mat], out.at[m, peer])
+
+    def finish(m, peer):
+        mat = m * parts + peer
+        w_ref[mat] = w_ref[mat] - learn_rate * back_ref[mat]
+        put(m, peer).start()
+
+    def add(m):
+        load(m, 2, slopes_ref, s_ref).wait()
+        load(m, 3, moments_ref, m_ref).wait()
+        some = pl.ds(m * parts, parts)
+        whole_ref[some] = hold_rate * m_ref[some] + s_ref[some]
+
+    add(0)
+    pl.semaphore_wait(barrier, parts + cols - 2)
+
+    @pl.loop(0, stages)
+    def _(m):
+        @pl.when(m > 0)
+        def _():
+            add(m)
+
+        for k in hops:
+            forward(m, lax.rem(f + parts + k * (1 - 2 * lax.rem(t, 2)), parts), f).start()
         take(m).start()
+        load(m, 4, whole_ref, momentum_ref).start()
+        load(m, 0, weights_ref, w_ref).start()
 
     dot = functools.partial(jnp.dot, precision=HIGH, preferred_element_type=jnp.float32)
 
@@ -84,7 +118,7 @@
     def _(m):
         take(m).wait()
         for k in hops:
-            peer = lax.rem(f + k, parts)
+            peer = lax.rem(f + parts + k * (1 - 2 * lax.rem(t, 2)), parts)
             forward(m, peer, peer).wait_recv()
         x = x_ref[m].reshape(side, wide)
         g_ref[m, t] = lax.dot_general(x, x, (((1,), (1,)), ((), ())), precision=HIGH, preferred_element_type=jnp.float32)
@@ -99,39 +133,70 @@
         total = polynomial(gram, dot, lambda a: jnp.sum(jnp.sum(a, axis=1, keepdims=True), axis=0, keepdims=True))
         y_ref[m] = dot(total, x_ref[m].reshape(side, wide)).reshape(parts, rows, wide)
         for k in hops:
-            backward(m, lax.rem(f + k, parts), f).start()
+            backward(m, lax.rem(f + parts + k * (1 - 2 * lax.rem(t, 2)), parts), f).start()
         give(m).start()
 
     @pl.loop(0, stages)
     def _(m):
         give(m).wait()
-        for k in hops:
-            peer = lax.rem(f + k, parts)
+        load(m, 0, weights_ref, w_ref).wait()
+        finish(m, f)
+        for k in hops:
+            peer = lax.rem(f + parts + k * (1 - 2 * lax.rem(t, 2)), parts)
+            backward(m, peer, peer).wait_recv()
+            finish(m, peer)
+
+    @pl.loop(0, stages)
+    def _(m):
+        load(m, 4, whole_ref, momentum_ref).wait()
+        put(m, f).wait()
+        for k in hops:
+            peer = lax.rem(f + parts + k * (1 - 2 * lax.rem(t, 2)), parts)
+            put(m, peer).wait()
             forward(m, peer, f).wait_send()
             backward(m, peer, f).wait_send()
-            backward(m, peer, peer).wait_recv()
         for k in range(1, cols):
             partial(m, lax.rem(t + k, cols), t).wait_send()
 
 
-def iterate_kernel(new_momentum, parts, cols):
-    mats, rows, wide = new_momentum.shape
+def leave(first_ref, second_ref, first_out, second_out, sems):
+    copies = [pltpu.make_async_copy(first_ref, first_out, sems.at[0]), pltpu.make_async_copy(second_ref, second_out, sems.at[1])]
+    for copy in copies:
+        copy.start()
+    for copy in copies:
+        copy.wait()
+
+
+def leave_kernel(first, second):
+    return pl.pallas_call(
+        leave,
+        out_shape=[jax.ShapeDtypeStruct(a.shape, a.dtype) for a in (first, second)],
+        in_specs=[pl.BlockSpec(memory_space=pl.ANY)] * 2,
+        out_specs=[pl.BlockSpec(memory_space=pl.ANY)] * 2,
+        scratch_shapes=[pltpu.SemaphoreType.DMA((2,))],
+        compiler_params=pltpu.CompilerParams(vmem_limit_bytes=2**20),
+    )(first, second)
+
+
+def iterate_kernel(slopes_in, moments_in, weights_in, parts, cols):
+    mats, rows, wide = slopes_in.shape
     stages, side = mats // parts, rows * parts
     dma = pltpu.SemaphoreType.DMA
     return pl.pallas_call(
         functools.partial(kernel, stages, parts, cols),
-        out_shape=jax.ShapeDtypeStruct(new_momentum.shape, new_momentum.dtype),
-        in_specs=[pl.BlockSpec(memory_space=pl.ANY)],
-        out_specs=pl.BlockSpec(memory_space=pl.ANY),
+        out_shape=[jax.ShapeDtypeStruct(slopes_in.shape, slopes_in.dtype)] * 2,
+        in_specs=[pl.BlockSpec(memory_space=pltpu.HBM)] * 3,
+        out_specs=[pl.BlockSpec(memory_space=pl.ANY)] * 2,
         scratch_shapes=[
+            *[pltpu.VMEM((mats, rows, wide), jnp.float32)] * 5,
             pltpu.VMEM((stages, parts, rows, wide), jnp.float32),
             pltpu.VMEM((stages, parts, rows, wide), jnp.float32),
             pltpu.VMEM((stages, cols, side, side), jnp.float32),
             dma((stages, parts)), dma((stages, parts)), dma((stages, parts)), dma((stages, parts)),
-            dma((stages, cols)), dma((stages, cols)), dma((2, stages)),
+            dma((stages, cols)), dma((stages, cols)), dma((6, stages)), dma((stages, parts)),
         ],
-        compiler_params=pltpu.CompilerParams(collective_id=0, has_side_effects=True),
-    )(new_momentum)
+        compiler_params=pltpu.CompilerParams(collective_id=0, has_side_effects=True, vmem_limit_bytes=48 * 2**20),
+    )(slopes_in, moments_in, weights_in)
 
 
 def iterate_plain(new_momentum):
@@ -143,12 +208,12 @@
 
 
 def body(parts, cols, slopes_in, moments_in, weights_in):
-    new_momentum = hold_rate * moments_in + slopes_in
-    if new_momentum.shape[1] % 8 == 0:
-        back = iterate_kernel(new_momentum, parts, cols)
+    if slopes_in.shape[1] % 8 == 0:
+        new_momentum, new_weights = iterate_kernel(slopes_in, moments_in, weights_in, parts, cols)
+        new_weights, new_momentum = leave_kernel(new_weights, new_momentum)
     else:
-        back = iterate_plain(new_momentum)
-    new_weights = weights_in - learn_rate * back
+        new_momentum = hold_rate * moments_in + slopes_in
+        new_weights = weights_in - learn_rate * iterate_plain(new_momentum)
     return (new_weights, new_momentum)
 
 

time: 106 us -> 101 us (0.953)
  other arithmetic: 7.46 us -> 0 us
  Pallas kernels: 97.3 us -> 100 us
    add x1 -> x0, other arithmetic: 4.16 us -> none  [body(): new_momentum = hold_rate * moments_in + slopes_in]
    sub x1 -> x0, other arithmetic: 3.3 us -> none  [body(): new_weights = weights_in - learn_rate * back]
    pallas_call x0 -> x1, Pallas kernels: none -> 2.03 us  [leave_kernel(): pl.pallas_call(leave, out_shape=[jax.ShapeDtypeStruct(a.shape, a.dtype) f...]
where the time goes in v3:
time: 101 us
  Pallas kernels  100 us (99%)
    pallas_call x1, Pallas kernels, iterate_kernel(): pl.pallas_call(functools.partial(kernel, stages, parts, cols), out_shape=...  98.1 us
    pallas_call x1, Pallas kernels, leave_kernel(): pl.pallas_call(leave, out_shape=[jax.ShapeDtypeStruct(a.shape, a.dtype) f...  2.03 us

profile of v3, /device:TPU:0, one launch (start us, length us, event | category | flops | bytes accessed | tf_op | source)
XLA Modules:
  0.0 100.7 jit_solution(4507042717028845678)
XLA Ops:
  0.6 98.1 %shard_map.50 = (f32[32,16,1024]{2,1,0:T(8,128)S(1)}, f32[32,16,1024]{2,1,0:T(8,128)S(1)}) custom-call(f32[32,16,1024]{2,1,0:T(8,128)} %slopes_ref.1, f32[32,16,1024]{2,1,0:T(8,128)} %moments_ref.1, f32[32,16,1024]{2,1,0:T(8,128)} %weights_ref.1), custom_call_target="tpu_custom_call" | custom-call | tf_op jit(solution)/shard_map/pallas_call | solution.py:185
  98.7 2.0 %shard_map.51 = (f32[32,16,1024]{2,1,0:T(8,128)}, f32[32,16,1024]{2,1,0:T(8,128)}) custom-call(f32[32,16,1024]{2,1,0:T(8,128)S(1)} %get-tuple-element.4.first_ref, f32[32,16,1024]{2,1,0:T(8,128)S(1)} %get-tuple-element.5.second_ref), custom_call_target="tpu_custom_call" | custom-call | tf_op jit(solution)/shard_map/pallas_call | solution.py:171
